TPU v7x, 128 devices: a whole 4x4x4 slice. The times are simulated.
128 devices in a mesh: atm: 8 (over z, core), land: 16 (over x, y).
Axes of the slice: x: 4, y: 4, z: 4, core: 2. Of those that a mesh axis runs over, the one named last changes fastest.
Arguments:
- tile_forcing: bfloat16 [16384, 128], P(('atm', 'land')), may hold values from -6 to 6
- elevation_gap: float32 [262144], P(('atm', 'land')), may hold values from -5 to 5
- lapse_rate: float32 [128], replicated, may hold values from -3 to 3
- column_tile: int32 [262144], P(('atm', 'land')), may hold values from 0 to 127
- column_target: int32 [262144], P(('atm', 'land')), may hold values from 0 to 655359, as said below
- owner_counts: int32 [128], P(('atm', 'land')), may hold values from 1 to 5120, as said below
- land_state: float32 [655360, 128], P(('atm', 'land')), may hold values from -6 to 6
- w_in: bfloat16 [256, 1024], replicated, may hold values from -0.375 to 0.375
- norm_gains: float32 [2, 1024], replicated, may hold values from 0.5 to 1.5
- w_up: bfloat16 [1, 1024, 1024], replicated, may hold values from -0.1875 to 0.1875
- w_down: bfloat16 [1, 1024, 1024], replicated, may hold values from -0.1875 to 0.1875
- w_out: bfloat16 [1024, 256], replicated, may hold values from -0.1875 to 0.1875
Outputs:
- new_state: float32 [655360, 128], P(('atm', 'land'))
- tile_flux: float32 [16384, 128], P(('atm', 'land'))
Inputs may be any that keep to these rules, and one draw needn't show every extreme that they name: `column_target`: live slots of owner j are j * 5120 to j * 5120 + owner_counts[j] - 1; every live slot is named by exactly one column and no other slot is named. The columns of one device name at most 41 slots of any one owner, and some pair reaches 41. `owner_counts`: they sum to 262144; the largest is exactly 5120. `column_tile`: index of the column's tile among the 128 tiles of the device that holds the column.
All inputs are finite; a program needn't handle non-finite values.
Results may differ from a plain program's by a relative error of at most 0.0038.
Values may be sent and summed in bfloat16 or wider, within the bound.
A program may use at most 128 MiB of HBM per device.

v0:
```python
import jax
import jax.numpy as jnp
from jax import lax
from jax.sharding import PartitionSpec as P


def as_sent(shard):

    def short(part):
        return part.astype(jnp.bfloat16) if part.dtype == jnp.float32 else part

    return jax.tree.map(short, shard)


def normed(hidden, gain):
    scale = lax.rsqrt(jnp.mean(hidden * hidden, axis=-1, keepdims=True) + 1e-06)
    return hidden * scale * gain


def network(inputs, w_in, norm_gains, w_up, w_down, w_out):
    hidden = jnp.dot(inputs, w_in, preferred_element_type=jnp.float32)
    lowered = normed(hidden, norm_gains[0]).astype(jnp.bfloat16)
    active = jax.nn.silu(jnp.dot(lowered, w_up[0], preferred_element_type=jnp.float32)).astype(
        jnp.bfloat16
    )
    hidden = hidden + jnp.dot(active, w_down[0], preferred_element_type=jnp.float32)
    lowered = normed(hidden, norm_gains[w_up.shape[0]]).astype(jnp.bfloat16)
    return jnp.dot(lowered, w_out, preferred_element_type=jnp.float32).astype(jnp.bfloat16)


def pick_rows(values, source):
    padded = jnp.concatenate([values, jnp.zeros((1,) + values.shape[1:], values.dtype)], axis=0)
    return jnp.take(padded, source, axis=0)


def inverse_map(places, length, empty):
    filler = jnp.full((length + 1,), empty, jnp.int32)
    return filler.at[places].set(jnp.arange(places.shape[0], dtype=jnp.int32))[:length]


def send_rows(values):
    devices = lax.axis_size(("atm", "land"))
    shaped = values.reshape((devices, -1) + values.shape[1:])
    moved = lax.all_to_all(
        as_sent(shaped), ("atm", "land"), split_axis=0, concat_axis=0, tiled=True
    ).astype(shaped.dtype)
    return moved.reshape(values.shape)


def local(
    tile_forcing,
    elevation_gap,
    lapse_rate,
    column_tile,
    column_target,
    owner_counts,
    land_state,
    w_in,
    norm_gains,
    w_up,
    w_down,
    w_out,
):
    devices = lax.axis_size(("atm", "land"))
    capacity = land_state.shape[0]
    per_peer = capacity // devices + 1
    columns = elevation_gap.shape[0]
    tiles = tile_forcing.shape[0]
    state_width = land_state.shape[1]
    tile_hot = (column_tile[:, None] == jnp.arange(tiles, dtype=jnp.int32)[None, :]).astype(
        jnp.bfloat16
    )
    looked = jnp.dot(tile_hot, tile_forcing, preferred_element_type=jnp.float32)
    column_forcing = (looked + elevation_gap[:, None] * lapse_rate[None, :]).astype(jnp.bfloat16)
    receiver = column_target // capacity
    local_slot = column_target % capacity
    peer_hot = (receiver[:, None] == jnp.arange(devices, dtype=jnp.int32)[None, :]).astype(
        jnp.int32
    )
    within = jnp.sum(jnp.cumsum(peer_hot, axis=0) * peer_hot, axis=1) - 1
    position = receiver * per_peer + within
    buffer_rows = devices * per_peer
    column_of_row = inverse_map(position, buffer_rows, columns)
    slot_buffer = jnp.where(
        column_of_row < columns, jnp.take(local_slot, jnp.minimum(column_of_row, columns - 1)), -1
    )
    living = jnp.arange(capacity, dtype=jnp.int32) < owner_counts[0]
    state_in = land_state.astype(jnp.bfloat16)
    got_slots = send_rows(slot_buffer)
    safe_slots = jnp.clip(got_slots, 0, capacity - 1)
    state_back = send_rows(jnp.take(state_in, safe_slots, axis=0))
    column_state = jnp.take(state_back, position, axis=0)
    inputs = jnp.concatenate([column_forcing, column_state], axis=1)
    result = network(inputs, w_in, norm_gains, w_up, w_down, w_out)
    tend_buffer = pick_rows(result[:, :state_width], column_of_row)
    got_tend = send_rows(tend_buffer)
    landing = jnp.where(got_slots >= 0, got_slots, capacity)
    row_of_slot = inverse_map(landing, capacity, buffer_rows)
    land_tend = pick_rows(got_tend, row_of_slot)
    new_state = jnp.where(
        living[:, None], land_state + land_tend.astype(jnp.float32), jnp.float32(0.0)
    )
    flux_column = result[:, state_width:]
    totals = jnp.dot(tile_hot.T, flux_column, preferred_element_type=jnp.float32)
    numbers = jnp.sum(tile_hot.astype(jnp.float32), axis=0)
    tile_flux = totals / jnp.maximum(numbers, 1.0)[:, None]
    return (new_state, tile_flux)


def solution(mesh):
    return jax.shard_map(
        local,
        mesh=mesh,
        in_specs=(
            P(("atm", "land"), None),
            P(("atm", "land")),
            P(),
            P(("atm", "land")),
            P(("atm", "land")),
            P(("atm", "land")),
            P(("atm", "land"), None),
            P(),
            P(),
            P(),
            P(),
            P(),
        ),
        out_specs=(P(("atm", "land"), None), P(("atm", "land"), None)),
        check_vma=False,
    )
```

profile of v0, /device:TPU:1, one launch (start us, length us, event | category | flops | bytes accessed | tf_op | source)
XLA Modules:
  0.0 237.4 jit_solution(7541502138396690324)
XLA Ops:
  3.7 8.1 %scatter_custom_fusion = s32[5249]{0:T(1024)S(1)} fusion(s32[2048]{0:T(1024)S(1)} %get-tuple-element.9, s32[2048]{0:T(1024)S(1)} %iota.21, s32[]{:T(128)} %constant.73.clone.1), kind=kCustom, calls=%fused_computation.74 | custom fusion | bytes 21000 | tf_op jit(solution)/shard_map/scatter | solution.py:38
  13.2 27.4 %gather_fusion = s32[5248]{0:T(1024)S(1)} fusion(s32[2048]{0:T(1024)S(1)} %get-tuple-element.12, s32[6144]{0:T(1024)S(1)} %get-tuple-element.20), kind=kCustom, calls=%fused_computation | custom fusion | bytes 62976 | tf_op jit(solution)/shard_map/jit(_take)/gather | solution.py:85
  41.7 11.5 %all-to-all-start = ((s32[128,1,41]{2,1,0:T(1,128)}), s32[128,1,41]{2,1,0:T(1,128)S(1)}, u32[]{:S(2)}, u32[]{:S(2)}) async-start(s32[128,1,41]{2,1,0:T(1,128)} %bitcast.5), calls=%async_computation | async-start | bytes 131072 | tf_op jit(solution)/shard_map/all_to_all | solution.py:44
  53.2 1.9 convert_element_type.34
  55.1 7.7 %all-to-all-done = s32[128,1,41]{2,1,0:T(1,128)S(1)} async-done(((s32[128,1,41]{2,1,0:T(1,128)}), s32[128,1,41]{2,1,0:T(1,128)S(1)}, u32[]{:S(2)}, u32[]{:S(2)}) %all-to-all-start) | async-done | bytes 21024 | tf_op jit(solution)/shard_map/all_to_all | solution.py:44
  65.1 11.6 %gather_fusion.1 = bf16[5248,128]{1,0:T(8,128)(2,1)} fusion(bf16[5120,128]{1,0:T(8,128)(2,1)S(1)} %convert_element_type.34, s32[6144]{0:T(1024)S(1)} %pad_clamp_fusion.1), kind=kCustom, calls=%fused_computation.1 | custom fusion | bytes 2707968 | tf_op jit(solution)/shard_map/jit(_take)/gather | solution.py:91
  76.7 3.3 %gather.29 = bf16[128,41,128]{2,1,0:T(8,128)(2,1)} reshape(bf16[5248,128]{1,0:T(8,128)(2,1)} %gather_fusion.1) | data formatting | bytes 2686976 | tf_op jit(solution)/shard_map/jit(_take)/gather | solution.py:91
  80.0 4.1 %broadcast_select_fusion = bf16[128,41,128]{2,1,0:T(8,128)(2,1)} fusion(bf16[128,41,128]{2,1,0:T(8,128)(2,1)} %gather.29, pred[128,41]{1,0:T(8,128)(4,1)S(1)} %copy-done.7), kind=kLoop, calls=%fused_computation.26 | loop fusion | flops 671744 | bytes 2692224 | tf_op jit(solution)/shard_map/jit(_take)/select_n | solution.py:91
  84.1 5.6 %all-to-all-start.1 = ((bf16[128,41,128]{2,1,0:T(8,128)(2,1)}), bf16[128,41,128]{2,1,0:T(8,128)(2,1)}, u32[]{:S(2)}, u32[]{:S(2)}) async-start(bf16[128,41,128]{2,1,0:T(8,128)(2,1)} %broadcast_select_fusion), calls=%async_computation.1 | async-start | bytes 3145728 | tf_op jit(solution)/shard_map/all_to_all | solution.py:44
  90.1 1.4 fusion.9
  91.5 22.2 %all-to-all-done.1 = bf16[128,41,128]{2,1,0:T(8,128)(2,1)} async-done(((bf16[128,41,128]{2,1,0:T(8,128)(2,1)}), bf16[128,41,128]{2,1,0:T(8,128)(2,1)}, u32[]{:S(2)}, u32[]{:S(2)}) %all-to-all-start.1) | async-done | bytes 1343520 | tf_op jit(solution)/shard_map/all_to_all | solution.py:44
  113.7 2.4 %reshape.206 = bf16[5248,128]{1,0:T(8,128)(2,1)S(1)} reshape(bf16[128,41,128]{2,1,0:T(8,128)(2,1)} %all-to-all-done.1) | data formatting | bytes 2686976 | tf_op jit(solution)/shard_map/reshape | solution.py:47
  116.1 8.1 %gather_fusion.2 = bf16[2048,128]{1,0:T(8,128)(2,1)} fusion(bf16[5248,128]{1,0:T(8,128)(2,1)S(1)} %reshape.206, s32[2048]{0:T(1024)S(1)} %copy-done.8), kind=kCustom, calls=%fused_computation.2 | custom fusion | bytes 1056768 | tf_op jit(solution)/shard_map/jit(_take)/gather | solution.py:92
  125.5 5.6 %multiply_reduce_fusion.1 = (f32[2048]{0:T(1024)S(1)}, f32[2048,1024]{0,1:T(8,128)}) fusion(bf16[256,1024]{1,0:T(8,128)(2,1)S(1)} %copy-done.1, bf16[2048,128]{0,1:T(8,128)(2,1)S(1)} %broadcast_select_fusion.2, bf16[2048,128]{0,1:T(8,128)(2,1)} %fusion.9), kind=kOutput, calls=%fused_computation.11 | convolution fusion | flops 1080031232 | bytes 9969664 | tf_op jit(solution)/shard_map/dot_general | solution.py:21
  131.1 16.6 %multiply_reduce_fusion = (f32[2048]{0:T(1024)S(1)}, f32[2048,1024]{0,1:T(8,128)}) fusion(f32[2048,1024]{0,1:T(8,128)} %get-tuple-element.16, bf16[1,1024,1024]{2,1,0:T(8,128)(2,1)S(1)} %copy-done, f32[1024]{0:T(1024)S(1)} %bitcast.38, f32[2048]{0:T(1024)S(1)} %add_rsqrt_fusion.1, bf16[1,1024,1024]{2,1,0:T(8,128)(2,1)} %param.21), kind=kOutput, calls=%fused_computation.8 | convolution fusion | flops 8613001216 | bytes 20992000 | tf_op jit(solution)/shard_map/dot_general | solution.py:26
  147.7 4.9 %fusion.8 = bf16[2048,256]{1,0:T(8,128)(2,1)S(1)} fusion(bf16[1024,256]{1,0:T(8,128)(2,1)S(1)} %copy-done.11, f32[2048,1024]{0,1:T(8,128)} %get-tuple-element.18, f32[1024]{0:T(1024)S(1)} %bitcast.37, f32[2048]{0:T(1024)S(1)} %add_rsqrt_fusion), kind=kOutput, calls=%fused_computation.21 | convolution fusion | flops 1080557568 | bytes 9973760 | tf_op jit(solution)/shard_map/dot_general | solution.py:28
  153.6 11.6 %gather_fusion.3 = bf16[5248,128]{1,0:T(8,128)(2,1)} fusion(bf16[2049,128]{1,0:T(8,128)(2,1)S(1)} %concatenate.10, s32[6144]{0:T(1024)S(1)} %copy-done.5), kind=kCustom, calls=%fused_computation.3 | custom fusion | bytes 2707968 | tf_op jit(solution)/shard_map/jit(_take)/gather | solution.py:33
  165.2 3.3 %gather.32 = bf16[128,41,128]{2,1,0:T(8,128)(2,1)} reshape(bf16[5248,128]{1,0:T(8,128)(2,1)} %gather_fusion.3) | data formatting | bytes 2686976 | tf_op jit(solution)/shard_map/jit(_take)/gather | solution.py:33
  168.5 4.1 %broadcast_select_fusion.1 = bf16[128,41,128]{2,1,0:T(8,128)(2,1)} fusion(bf16[128,41,128]{2,1,0:T(8,128)(2,1)} %gather.32, pred[128,41]{1,0:T(8,128)(4,1)S(1)} %compare_and_fusion.1), kind=kLoop, calls=%fused_computation.27 | loop fusion | flops 671744 | bytes 2692224 | tf_op jit(solution)/shard_map/jit(_take)/select_n | solution.py:33
  172.6 6.0 %all-to-all-start.2 = ((bf16[128,41,128]{2,1,0:T(8,128)(2,1)}), bf16[128,41,128]{2,1,0:T(8,128)(2,1)}, u32[]{:S(2)}, u32[]{:S(2)}) async-start(bf16[128,41,128]{2,1,0:T(8,128)(2,1)} %broadcast_select_fusion.1), calls=%async_computation.2 | async-start | bytes 3145728 | tf_op jit(solution)/shard_map/all_to_all | solution.py:44
  179.6 25.3 %scatter_custom_fusion.1 = s32[5121]{0:T(1024)S(1)} fusion(s32[5248]{0:T(1024)S(1)} %get-tuple-element.2, s32[5248]{0:T(1024)S(1)} %iota.22, s32[]{:T(128)} %constant.72.clone.1), kind=kCustom, calls=%fused_computation.76 | custom fusion | bytes 20488 | tf_op jit(solution)/shard_map/scatter | solution.py:38
  206.3 3.4 %reshape.207 = bf16[5248,128]{1,0:T(8,128)(2,1)} reshape(bf16[128,41,128]{2,1,0:T(8,128)(2,1)} %all-to-all-done.2) | data formatting | bytes 2686976 | tf_op jit(solution)/shard_map/reshape | solution.py:47
  211.1 18.6 %gather_fusion.4 = bf16[5120,128]{1,0:T(8,128)(2,1)} fusion(bf16[5249,128]{1,0:T(8,128)(2,1)S(1)} %concatenate.11, s32[5120]{0:T(1024)S(1)} %fusion.27), kind=kCustom, calls=%fused_computation.4 | custom fusion | bytes 2641920 | tf_op jit(solution)/shard_map/jit(_take)/gather | solution.py:33
  229.7 7.6 %add_select_fusion = f32[5120,128]{1,0:T(8,128)} fusion(f32[5120,128]{1,0:T(8,128)} %param.18, bf16[5120,128]{1,0:T(8,128)(2,1)} %gather_fusion.4, pred[5120]{0:T(1024)(128)(4,1)S(1)} %compare_and_fusion.2, pred[5120]{0:T(1024)(128)(4,1)S(1)} %iota_compare_fusion.6), kind=kLoop, calls=%fused_computation.20 | loop fusion | flops 2621440 | bytes 6563840 | tf_op jit(solution)/shard_map/jit(_where)/select_n | solution.py:100
  (73 shorter events, 13.6 us)
Async XLA Ops:
  0.6 130.4 %copy-start = (bf16[1,1024,1024]{2,1,0:T(8,128)(2,1)S(1)}, bf16[1,1024,1024]{2,1,0:T(8,128)(2,1)}, u32[]{:S(2)}) copy-start(bf16[1,1024,1024]{2,1,0:T(8,128)(2,1)} %param.22) | copy-start | bytes 6291460
  2.1 1.0 copy-start.6
  41.7 21.0 %all-to-all-start = ((s32[128,1,41]{2,1,0:T(1,128)}), s32[128,1,41]{2,1,0:T(1,128)S(1)}, u32[]{:S(2)}, u32[]{:S(2)}) async-start(s32[128,1,41]{2,1,0:T(1,128)} %bitcast.5), calls=%async_computation | async-start | bytes 131072 | tf_op jit(solution)/shard_map/all_to_all | solution.py:44
  76.7 3.3 %copy-start.7 = (pred[128,41]{1,0:T(8,128)(4,1)S(1)}, pred[128,41]{1,0:T(8,128)(4,1)}, u32[]{:S(2)}) copy-start(pred[128,41]{1,0:T(8,128)(4,1)} %compare_and_fusion) | copy-start | bytes 15748
  84.1 5.6 %copy-start.4 = (s32[5248]{0:T(1024)S(1)}, s32[5248]{0:T(1024)}, u32[]{:S(2)}) copy-start(s32[5248]{0:T(1024)} %get-tuple-element.4) | copy-start | bytes 62980
  84.1 5.8 %copy-start.9 = (f32[2,1024]{1,0:T(2,128)S(1)}, f32[2,1024]{1,0:T(2,128)}, u32[]{:S(2)}) copy-start(f32[2,1024]{1,0:T(2,128)} %param.20) | copy-start | bytes 24580
  84.1 5.9 %copy-start.10 = (s32[2048]{0:T(1024)S(1)}, s32[2048]{0:T(1024)}, u32[]{:S(2)}) copy-start(s32[2048]{0:T(1024)} %param.15) | copy-start | bytes 24580
  84.1 5.9 %copy-start.12 = (bf16[128,128]{1,0:T(8,128)(2,1)S(1)}, bf16[128,128]{1,0:T(8,128)(2,1)}, u32[]{:S(2)}) copy-start(bf16[128,128]{1,0:T(8,128)(2,1)} %param.12) | copy-start | bytes 98308
  84.1 5.9 %copy-start.13 = (f32[2048]{0:T(1024)S(1)}, f32[2048]{0:T(1024)}, u32[]{:S(2)}) copy-start(f32[2048]{0:T(1024)} %param.13) | copy-start | bytes 24580
  84.1 5.9 %copy-start.14 = (f32[128]{0:T(128)S(1)}, f32[128]{0:T(128)}, u32[]{:S(2)}) copy-start(f32[128]{0:T(128)} %param.14) | copy-start | bytes 1540
  84.1 29.5 %all-to-all-start.1 = ((bf16[128,41,128]{2,1,0:T(8,128)(2,1)}), bf16[128,41,128]{2,1,0:T(8,128)(2,1)}, u32[]{:S(2)}, u32[]{:S(2)}) async-start(bf16[128,41,128]{2,1,0:T(8,128)(2,1)} %broadcast_select_fusion), calls=%async_computation.1 | async-start | bytes 3145728 | tf_op jit(solution)/shard_map/all_to_all | solution.py:44
  89.7 26.3 %copy-start.8 = (s32[2048]{0:T(1024)S(1)}, s32[2048]{0:T(1024)}, u32[]{:S(2)}) copy-start(s32[2048]{0:T(1024)} %get-tuple-element.8) | copy-start | bytes 24580
  124.1 1.4 copy-start.1
  131.1 16.6 %copy-start.11 = (bf16[1024,256]{1,0:T(8,128)(2,1)S(1)}, bf16[1024,256]{1,0:T(8,128)(2,1)}, u32[]{:S(2)}) copy-start(bf16[1024,256]{1,0:T(8,128)(2,1)} %param.23) | copy-start | bytes 1572868
  152.6 1.0 copy-start.2
  152.6 1.0 copy-start.5
  172.6 32.4 %copy-start.3 = (bf16[2048,256]{1,0:T(8,128)(2,1)S(1)}, bf16[2048,256]{1,0:T(8,128)(2,1)}, u32[]{:S(2)}) copy-start(bf16[2048,256]{1,0:T(8,128)(2,1)} %copy-done.2) | copy-start | bytes 3145732
  172.6 33.7 %all-to-all-start.2 = ((bf16[128,41,128]{2,1,0:T(8,128)(2,1)}), bf16[128,41,128]{2,1,0:T(8,128)(2,1)}, u32[]{:S(2)}, u32[]{:S(2)}) async-start(bf16[128,41,128]{2,1,0:T(8,128)(2,1)} %broadcast_select_fusion.1), calls=%async_computation.2 | async-start | bytes 3145728 | tf_op jit(solution)/shard_map/all_to_all | solution.py:44
where the time goes:
time: 238 us; the launch traced here: 237 us
  local copies, waits for them, and re-layouts  129 us (54%)
  matrix products  29.9 us (13%)
  waiting for transfers between devices  29.8 us (13%)
  other arithmetic  24.2 us (10%)
  starting transfers between devices  23 us (10%)
    gather x3, local copies, waits for them, and re-layouts, pick_rows(): return jnp.take(padded, source, axis=0)  33.5 us
    scatter x2, local copies, waits for them, and re-layouts, inverse_map(): filler.at[places].set(jnp.arange(places.shape[0], dtype=jnp.int32))[:length]  33.4 us
    all_to_all x3, waiting for transfers between devices, send_rows(): lax.all_to_all(as_sent(shaped), ('atm', 'land'), split_axis=0, concat_axi...  29.8 us
    gather x2, local copies, waits for them, and re-layouts, local(): jnp.take(local_slot, jnp.minimum(column_of_row, columns - 1))  27.6 us
    all_to_all x3, starting transfers between devices, send_rows(): lax.all_to_all(as_sent(shaped), ('atm', 'land'), split_axis=0, concat_axi...  23 us
    dot_general x1, matrix products, network(): jnp.dot(active, w_down[0], preferred_element_type=jnp.float32)  16.6 us
    gather x2, local copies, waits for them, and re-layouts, local(): state_back = send_rows(jnp.take(state_in, safe_slots, axis=0))  14.9 us
    gather x2, local copies, waits for them, and re-layouts, local(): column_state = jnp.take(state_back, position, axis=0)  9.35 us
  transfers between devices with their start and end apart: 3, of which 2 were waited for; matrix products, arithmetic and copies ran while one was open for 13% of the time, Pallas kernels for 0%

commit v1 on v0

v1 whole, which is shorter than its diff:
```python
import functools

import jax
import jax.numpy as jnp
from jax import lax
from jax.experimental import pallas as pl
from jax.experimental.pallas import tpu as pltpu
from jax.sharding import PartitionSpec as P

F32 = jnp.float32
BF16 = jnp.bfloat16
LANES = 128
VMEM = pl.BlockSpec(memory_space=pltpu.VMEM)
SMEM = pl.BlockSpec(memory_space=pltpu.SMEM)
ANY = pl.BlockSpec(memory_space=pl.ANY)
MESH = pl.DeviceIdType.MESH


def dot(a, b):
    return jnp.dot(a, b, preferred_element_type=F32)


def dot_nt(a, b):
    return lax.dot_general(a, b, (((1,), (1,)), ((), ())), preferred_element_type=F32)


def dot_tn(a, b):
    return lax.dot_general(a, b, (((0,), (0,)), ((), ())), preferred_element_type=F32)


def iota(shape, dim):
    return lax.broadcasted_iota(jnp.int32, shape, dim)


def hot(mask):
    return jnp.where(mask, 1.0, 0.0)


def prep_kernel(
    n, per_peer, rows, capacity, tf_ref, gap_ref, lapse_ref, tile_ref, target_ref,
    send_ref, slots_ref, hots_ref, counts_ref,
):
    columns = target_ref.shape[1]
    tiles = tf_ref.shape[0]
    target = target_ref[...].astype(F32)
    owner_f = jnp.floor((target + 0.5) * (1.0 / capacity))
    slot_p = target - owner_f * capacity + 1.0
    owner = owner_f.astype(jnp.int32)
    owner_hot = hot(iota((n, columns), 0) == owner)
    owner_bf = owner_hot.astype(BF16)
    block = min(256, columns)
    upper = hot(iota((block, block), 0) <= iota((block, block), 1)).astype(BF16)
    running = jnp.zeros((n, 1), F32)
    ranks = []
    for b in range(columns // block):
        part = slice(b * block, (b + 1) * block)
        seen = dot(owner_bf[:, part], upper)
        ranks.append(jnp.sum(owner_hot[:, part] * (seen + running), axis=0, keepdims=True) - 1.0)
        running = running + seen[:, block - 1 : block]
    rank = jnp.concatenate(ranks, axis=1).astype(jnp.int32)
    place = hot(iota((LANES, columns), 0) == rank)
    high = jnp.floor(slot_p * (1.0 / 64.0))
    low = slot_p - 64.0 * high
    slot_hi = dot_nt(owner_bf, (place * high).astype(BF16))
    slot_lo = dot_nt(owner_bf, (place * low).astype(BF16))
    slot = slot_hi * 64.0 + slot_lo - 1.0
    slots_ref[...] = jnp.where(slot < 0.0, float(capacity), slot).astype(jnp.int32)
    tile = tile_ref[...]
    gap = gap_ref[...]
    gap_1 = gap.astype(BF16).astype(F32)
    gap_2 = (gap - gap_1).astype(BF16).astype(F32)
    gap_3 = gap - gap_1 - gap_2
    short = place[:rows]
    tile_of = dot_nt((short * (tile.astype(F32) + 1.0)).astype(BF16), owner_bf)
    gap_of = (
        dot_nt((short * gap_1).astype(BF16), owner_bf)
        + dot_nt((short * gap_2).astype(BF16), owner_bf)
    ) + dot_nt((short * gap_3).astype(BF16), owner_bf)
    number = jnp.sum(hot(iota((tiles, columns), 0) == tile), axis=1, keepdims=True)
    counts_ref[...] = jnp.broadcast_to(jnp.maximum(number, 1.0), counts_ref.shape)
    group = min(16, n)
    lapse = lapse_ref[...]
    table = tf_ref[...]
    lane = iota((rows, tiles), 1).astype(F32) + 1.0

    def body(b, carry):
        tile_now, gap_now = carry
        hots = jnp.concatenate(
            [hot(lane == tile_now[:, i : i + 1]).astype(BF16) for i in range(group)], axis=0
        )
        lifts = jnp.concatenate([gap_now[:, i : i + 1] * lapse for i in range(group)], axis=0)
        forcing = (dot(hots, table) + lifts).astype(BF16)
        spot = pl.ds(b * group, group)
        hots_ref[spot] = hots.reshape(group, rows, tiles)
        send_ref[spot] = forcing.reshape(group, rows, LANES)
        return (
            pltpu.roll(tile_now, n - group, axis=1) if n > group else tile_now,
            pltpu.roll(gap_now, n - group, axis=1) if n > group else gap_now,
        )

    lax.fori_loop(0, n // group, body, (tile_of, gap_of))


def net(x_ref, hid, low, act, gains, w_in, w_up, w_down, w_out, width):
    hidden = hid.shape[1]
    parts = [slice(i * width, (i + 1) * width) for i in range(hidden // width)]
    x = x_ref[...]
    total = None
    for c in parts:
        h = dot(x, w_in[:, c])
        hid[:, c] = h
        low[:, c] = (h * gains[0:1, c]).astype(BF16)
        s = jnp.sum(h * h, axis=1, keepdims=True)
        total = s if total is None else total + s
    half = lax.rsqrt(total * (1.0 / hidden) + 1e-6) * 0.5
    for c in parts:
        v = dot(low[...], w_up[:, c]) * half
        act[:, c] = (v + v * jnp.tanh(v)).astype(BF16)
    total = None
    for c in parts:
        h = hid[:, c] + dot(act[...], w_down[:, c])
        low[:, c] = (h * gains[1:2, c]).astype(BF16)
        s = jnp.sum(h * h, axis=1, keepdims=True)
        total = s if total is None else total + s
    scale = lax.rsqrt(total * (1.0 / hidden) + 1e-6)
    return dot(low[...], w_out[...]) * scale


def main_kernel(
    sizes, per_peer, rows, capacity, group, width,
    send_ref, slots_ref, land_ref, gains_ref, w_in_ref, w_up_ref, w_down_ref, w_out_ref,
    fresh_ref, got_slots, flux_ref,
    got, slots_s, land, w_in, w_up, w_down, w_out, state, forcing, x, hid, low, act, flux, back,
    load_sem, slot_send, slot_recv, send_sem, recv_sem, back_send, back_recv, smem_sem,
):
    n_atm, n_land = sizes
    n = n_atm * n_land
    atm = lax.axis_index("atm")
    lnd = lax.axis_index("land")
    me = atm * n_land + lnd
    block = group * per_peer

    def ahead(d):
        return lax.rem(atm + d // n_land, n_atm), lax.rem(lnd + lax.rem(d, n_land), n_land)

    def behind(d):
        return (
            lax.rem(atm - d // n_land + n_atm, n_atm),
            lax.rem(lnd - lax.rem(d, n_land) + n_land, n_land),
        )

    barrier = pltpu.get_barrier_semaphore()

    def greet(d, carry):
        pl.semaphore_signal(barrier, inc=1, device_id=ahead(d), device_id_type=MESH)
        return carry

    lax.fori_loop(1, n, greet, 0)
    loads = [
        pltpu.make_async_copy(src, dst, load_sem.at[i])
        for i, (src, dst) in enumerate(
            [
                (land_ref, land.at[pl.ds(0, capacity)]),
                (w_in_ref, w_in),
                (w_up_ref, w_up),
                (w_down_ref, w_down),
                (w_out_ref, w_out),
            ]
        )
    ]
    for load in loads:
        load.start()
    land[pl.ds(capacity, 8), :] = jnp.zeros((8, LANES), F32)
    flux[pl.ds(block, 8), :] = jnp.zeros((8, LANES), F32)
    got_slots[0] = slots_ref[me]
    got[0] = send_ref[me]
    pl.semaphore_wait(barrier, n - 1)

    def slot_copy(d):
        a, b = ahead(d)
        return pltpu.make_async_remote_copy(
            src_ref=slots_ref.at[a * n_land + b], dst_ref=got_slots.at[d],
            send_sem=slot_send, recv_sem=slot_recv, device_id=(a, b), device_id_type=MESH,
        )

    def forcing_copy(d):
        a, b = ahead(d)
        return pltpu.make_async_remote_copy(
            src_ref=send_ref.at[a * n_land + b], dst_ref=got.at[d],
            send_sem=send_sem, recv_sem=recv_sem.at[d // group], device_id=(a, b), device_id_type=MESH,
        )

    def start_slots(d, carry):
        slot_copy(d).start()
        return carry

    def start_forcing(d, carry):
        forcing_copy(d).start()
        return carry

    lax.fori_loop(1, n, start_slots, 0)
    lax.fori_loop(1, n, start_forcing, 0)

    def many(ref, start, count, send, recv):
        spot = ref.at[pl.ds(start, count)]
        return pltpu.make_async_remote_copy(
            src_ref=spot, dst_ref=spot, send_sem=send, recv_sem=recv,
            device_id=ahead(1), device_id_type=MESH,
        )

    many(got_slots, 1, n - 1, slot_send, slot_recv).wait_recv()
    to_smem = pltpu.make_async_copy(got_slots, slots_s, smem_sem)
    to_smem.start()
    to_smem.wait()
    for load in loads:
        load.wait()

    def chunk(g, carry):
        first = g * group

        @pl.when(g == 0)
        def _():
            many(got, 1, group - 1, send_sem, recv_sem.at[0]).wait_recv()

        @pl.when(g > 0)
        def _():
            many(got, first, group, send_sem, recv_sem.at[g]).wait_recv()

        for p in range(group):
            for k in range(per_peer):
                slot = slots_s[first + p, 0, k]
                state[pl.ds(p * per_peer + k, 1), :] = land[pl.ds(slot, 1), :]
            forcing[pl.ds(p * per_peer, per_peer), :] = got[first + p, :per_peer, :].astype(F32)
        x[:, :LANES] = forcing[...].astype(BF16)
        x[:, LANES:] = state[...].astype(BF16)
        result = net(x, hid, low, act, gains_ref, w_in, w_up, w_down, w_out, width)
        tendency = result[:, :LANES].astype(BF16).astype(F32)
        fresh_ref[pl.ds(pl.multiple_of(g * block, 8), block), :] = state[...] + tendency
        flux[pl.ds(0, block), :] = result[:, LANES:]
        for p in range(group):
            back[first + p] = flux[pl.ds(p * per_peer, rows), :].astype(BF16)

        def give(p, carry):
            d = first + p

            @pl.when(d > 0)
            def _():
                pltpu.make_async_remote_copy(
                    src_ref=back.at[d], dst_ref=flux_ref.at[me],
                    send_sem=back_send, recv_sem=back_recv, device_id=behind(d), device_id_type=MESH,
                ).start()

            return carry

        lax.fori_loop(0, group, give, 0)
        return carry

    lax.fori_loop(0, n // group, chunk, 0)
    flux_ref[me] = back[0]
    many(got_slots, 1, n - 1, slot_send, slot_recv).wait_send()
    many(got, 1, n - 1, send_sem, recv_sem.at[0]).wait_send()
    many(back, 1, n - 1, back_send, back_recv).wait_send()
    many(back, 1, n - 1, back_send, back_recv).wait_recv()


def finish_kernel(n, per_peer, capacity, slots_ref, fresh_ref, flux_ref, hots_ref, counts_ref,
                  state_ref, tile_ref, out, sem):
    def clear(i, carry):
        out[pl.ds(i * 64, 64), :] = jnp.zeros((64, LANES), F32)
        return carry

    lax.fori_loop(0, capacity // 64, clear, 0)
    if capacity % 64:
        out[pl.ds(capacity // 64 * 64, capacity % 64), :] = jnp.zeros((capacity % 64, LANES), F32)

    def place(d, carry):
        for k in range(per_peer):
            slot = slots_ref[d, 0, k]
            out[pl.ds(slot, 1), :] = fresh_ref[pl.ds(d * per_peer + k, 1), :]
        return carry

    lax.fori_loop(0, n, place, 0)
    copy = pltpu.make_async_copy(out.at[pl.ds(0, capacity)], state_ref, sem)
    copy.start()
    total = hots_ref.shape[0]
    step = total // 8
    acc = None
    for i in range(8):
        part = slice(i * step, (i + 1) * step)
        t = dot_tn(hots_ref[part, :], flux_ref[part, :])
        acc = t if acc is None else acc + t
    tile_ref[...] = acc / counts_ref[...]
    copy.wait()


def limit(mib):
    return pltpu.CompilerParams(vmem_limit_bytes=mib * 1024 * 1024)


def local(
    sizes, tile_forcing, elevation_gap, lapse_rate, column_tile, column_target, owner_counts,
    land_state, w_in, norm_gains, w_up, w_down, w_out,
):
    n = sizes[0] * sizes[1]
    capacity = land_state.shape[0]
    per_peer = capacity // n + 1
    rows = -(-per_peer // 16) * 16
    columns = elevation_gap.shape[0]
    tiles, features = tile_forcing.shape
    hidden = w_in.shape[1]
    group = 16 if n % 16 == 0 else 2
    block = group * per_peer
    S = jax.ShapeDtypeStruct
    send, slots, hots, counts = pl.pallas_call(
        functools.partial(prep_kernel, n, per_peer, rows, capacity),
        out_shape=[
            S((n, rows, features), BF16), S((n, LANES), jnp.int32),
            S((n, rows, tiles), BF16), S((tiles, features), F32),
        ],
        in_specs=[VMEM] * 5,
        out_specs=[VMEM] * 4,
        compiler_params=limit(48),
        name="prep",
    )(
        tile_forcing, elevation_gap.reshape(1, columns), lapse_rate.reshape(1, features),
        column_tile.reshape(1, columns), column_target.reshape(1, columns),
    )
    slots = slots.reshape(n, 1, LANES)
    dma = pltpu.SemaphoreType.DMA
    fresh, got_slots, flux = pl.pallas_call(
        functools.partial(main_kernel, sizes, per_peer, rows, capacity, group, 256),
        out_shape=[
            S((n * per_peer, features), F32), S((n, 1, LANES), jnp.int32), S((n, rows, features), BF16),
        ],
        in_specs=[VMEM, VMEM, ANY, VMEM, ANY, ANY, ANY, ANY],
        out_specs=[VMEM] * 3,
        scratch_shapes=[
            pltpu.VMEM((n, rows, features), BF16),
            pltpu.SMEM((n, 1, LANES), jnp.int32),
            pltpu.VMEM((capacity + 8, features), F32),
            pltpu.VMEM(w_in.shape, BF16),
            pltpu.VMEM(w_up.shape[1:], BF16),
            pltpu.VMEM(w_down.shape[1:], BF16),
            pltpu.VMEM(w_out.shape, BF16),
            pltpu.VMEM((block, features), F32),
            pltpu.VMEM((block, features), F32),
            pltpu.VMEM((block, 2 * features), BF16),
            pltpu.VMEM((block, hidden), F32),
            pltpu.VMEM((block, hidden), BF16),
            pltpu.VMEM((block, hidden), BF16),
            pltpu.VMEM((block + 8, features), F32),
            pltpu.VMEM((n, rows, features), BF16),
            dma((5,)), dma(()), dma(()), dma(()), dma((n // group,)), dma(()), dma(()), dma(()),
        ],
        compiler_params=pltpu.CompilerParams(
            collective_id=0, has_side_effects=True, vmem_limit_bytes=60 * 1024 * 1024
        ),
        name="exchange",
    )(send, slots, land_state, norm_gains, w_in, w_up[0], w_down[0], w_out)
    return pl.pallas_call(
        functools.partial(finish_kernel, n, per_peer, capacity),
        out_shape=[S((capacity, features), F32), S((tiles, features), F32)],
        in_specs=[SMEM, VMEM, VMEM, VMEM, VMEM],
        out_specs=[ANY, VMEM],
        scratch_shapes=[pltpu.VMEM((capacity + 8, features), F32), dma(())],
        compiler_params=limit(32),
        name="finish",
    )(
        got_slots, fresh, flux.reshape(n * rows, features), hots.reshape(n * rows, tiles), counts
    )


def solution(mesh):
    both = P(("atm", "land"))
    wide = P(("atm", "land"), None)
    sizes = (mesh.shape["atm"], mesh.shape["land"])
    return jax.shard_map(
        functools.partial(local, sizes),
        mesh=mesh,
        in_specs=(wide, both, P(), both, both, both, wide, P(), P(), P(), P(), P()),
        out_specs=(wide, wide),
        check_vma=False,
    )
```

time: 238 us -> 94.5 us (0.40)
  local copies, waits for them, and re-layouts: 129 us -> 9.26 us
  Pallas kernels: 0 us -> 84 us
  matrix products: 29.9 us -> 0 us
  waiting for transfers between devices: 29.8 us -> 0 us
  other arithmetic: 24.2 us -> 0 us
  starting transfers between devices: 23 us -> 0 us
    gather x9 -> x0, local copies, waits for them, and re-layouts: 85.4 us -> none  [the longest x3 33.5 us: pick_rows(): return jnp.take(padded, source, axis=0)]
    pallas_call x0 -> x3, Pallas kernels: none -> 84 us  [the longest x1 70.4 us: local(): pl.pallas_call(functools.partial(main_kernel, sizes, per_peer, rows, capa...]
    scatter x2 -> x0, local copies, waits for them, and re-layouts: 33.4 us -> none  [inverse_map(): filler.at[places].set(jnp.arange(places.shape[0], dtype=jnp.int32))[:length]]
    dot_general x5 -> x0, matrix products: 29.9 us -> none  [the longest x1 16.6 us: network(): jnp.dot(active, w_down[0], preferred_element_type=jnp.float32)]
    all_to_all x3 -> x0, waiting for transfers between devices: 29.8 us -> none  [send_rows(): lax.all_to_all(as_sent(shaped), ('atm', 'land'), split_axis=0, concat_axi...]
    all_to_all x3 -> x0, starting transfers between devices: 23 us -> none  [send_rows(): lax.all_to_all(as_sent(shaped), ('atm', 'land'), split_axis=0, concat_axi...]
    select_n x7 -> x0, other arithmetic: 17.5 us -> none  [the longest x1 7.63 us: local(): jnp.where(living[:, None], land_state + land_tend.astype(jnp.float32), jn...]
    unnamed x30 -> x20, local copies, waits for them, and re-layouts: 0.93 us -> 9.26 us
  transfers between devices with their start and end apart: 3 -> 0, of which waited for: 2 -> 0; matrix products, arithmetic and copies ran while one was open for 13% -> 0% of each run, Pallas kernels for 0% -> 0%
where the time goes in v1:
time: 94.5 us; the launch traced here: 93.9 us
  Pallas kernels  84 us (89%)
  local copies, waits for them, and re-layouts  9.26 us (10%)
    pallas_call x1, Pallas kernels, local(): pl.pallas_call(functools.partial(main_kernel, sizes, per_peer, rows, capa...  70.4 us
    pallas_call x1, Pallas kernels, local(): pl.pallas_call(functools.partial(finish_kernel, n, per_peer, capacity), o...  9.36 us
    unnamed x20, local copies, waits for them, and re-layouts  9.26 us
    pallas_call x1, Pallas kernels, local(): pl.pallas_call(functools.partial(prep_kernel, n, per_peer, rows, capacity...  4.24 us

profile of v1, /device:TPU:1, one launch (start us, length us, event | category | flops | bytes accessed | tf_op | source)
XLA Modules:
  0.0 93.9 jit_solution(6298583872410421838)
XLA Ops:
  0.6 0.0 copy-start.5
  0.6 0.7 copy-done.5
  1.4 0.0 copy-start.6
  1.4 0.7 copy-done.6
  2.1 0.0 copy-start.7
  2.1 0.7 copy-done.7
  2.8 0.0 copy-start.8
  2.8 0.7 copy-done.8
  3.5 0.0 copy-start.9
  3.5 0.7 copy-done.9
  4.1 4.2 %prep.1 = (bf16[128,48,128]{2,1,0:T(8,128)(2,1)S(1)}, s32[128,128]{1,0:T(8,128)S(1)}, bf16[128,48,128]{2,1,0:T(8,128)(2,1)S(1)}, f32[128,128]{1,0:T(8,128)S(1)}) custom-call(bf16[128,128]{1,0:T(8,128)(2,1)S(1)} %copy-done.5, f32[1,2048]{1,0:T(1,128)S(1)} %bitcast.12, f32[1,128]{1,0:T(1,128)S(1)} %bitcast.15, s32[1,2048]{1,0:T(1,128)S(1)} %bitcast.13, ...), custom_call_target="tpu_custom_call" | custom-call | tf_op jit(solution)/shard_map/prep/pallas_call | solution.py:314
  8.4 0.0 copy-start.2
  8.4 1.1 %copy-done.2 = bf16[128,48,128]{2,1,0:T(8,128)(2,1)} copy-done((bf16[128,48,128]{2,1,0:T(8,128)(2,1)}, bf16[128,48,128]{2,1,0:T(8,128)(2,1)S(1)}, u32[]{:S(2)}) %copy-start.2) | copy-done | bytes 1572888
  9.5 0.0 copy-start.4
  9.5 0.6 copy-done.4
  10.2 70.4 %exchange.1 = (f32[5248,128]{1,0:T(8,128)}, s32[128,1,128]{2,1,0:T(1,128)}, bf16[128,48,128]{2,1,0:T(8,128)(2,1)}) custom-call(bf16[128,48,128]{2,1,0:T(8,128)(2,1)} %copy-done.2, s32[128,1,128]{2,1,0:T(1,128)} %bitcast.11, f32[5120,128]{1,0:T(8,128)} %land_ref.1, f32[2,1024]{1,0:T(2,128)} %gains_ref.1, bf16[256,1024]{1,0:T(8,128)(2,1)} %w_in_ref.1, ...), custom_call_target="tpu_custom_call" | custom-call | tf_op jit(solution)/shard_map/exchange/pallas_call | solution.py:330
  80.5 0.0 copy-start
  80.5 1.7 %copy-done = f32[5248,128]{1,0:T(8,128)S(1)} copy-done((f32[5248,128]{1,0:T(8,128)S(1)}, f32[5248,128]{1,0:T(8,128)}, u32[]{:S(2)}) %copy-start) | copy-done | bytes 2687000
  82.3 0.0 copy-start.1
  82.3 1.4 %copy-done.1 = bf16[128,48,128]{2,1,0:T(8,128)(2,1)S(1)} copy-done((bf16[128,48,128]{2,1,0:T(8,128)(2,1)S(1)}, bf16[128,48,128]{2,1,0:T(8,128)(2,1)}, u32[]{:S(2)}) %copy-start.1) | copy-done | bytes 1572888
  83.7 0.0 copy-start.3
  83.7 0.8 copy-done.3
  84.5 9.4 %finish.1 = (f32[5120,128]{1,0:T(8,128)}, f32[128,128]{1,0:T(8,128)}) custom-call(s32[128,1,128]{2,1,0:T(1,128)S(1)} %copy-done.3, f32[5248,128]{1,0:T(8,128)S(1)} %copy-done, bf16[6144,128]{1,0:T(8,128)(2,1)S(1)} %bitcast.10, bf16[6144,128]{1,0:T(8,128)(2,1)S(1)} %bitcast.9, f32[128,128]{1,0:T(8,128)S(1)} %get-tuple-element.15.counts_ref), custom_call_target="tpu_custom_call" | custom-call | tf_op jit(solution)/shard_map/finish/pallas_call | solution.py:360
Async XLA Ops:
  0.6 0.8 copy-start.5
  1.4 0.7 copy-start.6
  2.1 0.7 copy-start.7
  2.8 0.7 copy-start.8
  3.5 0.7 copy-start.9
  8.4 1.1 %copy-start.2 = (bf16[128,48,128]{2,1,0:T(8,128)(2,1)}, bf16[128,48,128]{2,1,0:T(8,128)(2,1)S(1)}, u32[]{:S(2)}) copy-start(bf16[128,48,128]{2,1,0:T(8,128)(2,1)S(1)} %get-tuple-element.9.send_ref) | copy-start | bytes 4718596
  9.5 0.6 copy-start.4
  80.5 1.8 %copy-start = (f32[5248,128]{1,0:T(8,128)S(1)}, f32[5248,128]{1,0:T(8,128)}, u32[]{:S(2)}) copy-start(f32[5248,128]{1,0:T(8,128)} %get-tuple-element.12.fresh_ref) | copy-start | bytes 8060932
  82.3 1.4 %copy-start.1 = (bf16[128,48,128]{2,1,0:T(8,128)(2,1)S(1)}, bf16[128,48,128]{2,1,0:T(8,128)(2,1)}, u32[]{:S(2)}) copy-start(bf16[128,48,128]{2,1,0:T(8,128)(2,1)} %get-tuple-element.13) | copy-start | bytes 4718596
  83.7 0.8 copy-start.3

commit v2 on v1

--- a/solution.py
+++ b/solution.py
@@ -11,7 +11,7 @@
 BF16 = jnp.bfloat16
 LANES = 128
 VMEM = pl.BlockSpec(memory_space=pltpu.VMEM)
-SMEM = pl.BlockSpec(memory_space=pltpu.SMEM)
+HBM = pl.BlockSpec(memory_space=pltpu.HBM)
 ANY = pl.BlockSpec(memory_space=pl.ANY)
 MESH = pl.DeviceIdType.MESH
 
@@ -36,7 +36,7 @@
     return jnp.where(mask, 1.0, 0.0)
 
 
-def prep_kernel(
+def prepare(
     n, per_peer, rows, capacity, tf_ref, gap_ref, lapse_ref, tile_ref, target_ref,
     send_ref, slots_ref, hots_ref, counts_ref,
 ):
@@ -64,7 +64,9 @@
     slot_hi = dot_nt(owner_bf, (place * high).astype(BF16))
     slot_lo = dot_nt(owner_bf, (place * low).astype(BF16))
     slot = slot_hi * 64.0 + slot_lo - 1.0
-    slots_ref[...] = jnp.where(slot < 0.0, float(capacity), slot).astype(jnp.int32)
+    slot = jnp.where(slot < 0.0, float(capacity), slot).astype(jnp.int32)
+    for j in range(n):
+        slots_ref[j] = slot[j : j + 1, :]
     tile = tile_ref[...]
     gap = gap_ref[...]
     gap_1 = gap.astype(BF16).astype(F32)
@@ -101,7 +103,7 @@
     lax.fori_loop(0, n // group, body, (tile_of, gap_of))
 
 
-def net(x_ref, hid, low, act, gains, w_in, w_up, w_down, w_out, width):
+def net(x_ref, hid, low, act, gains, w_in, w_up, w_down, w_out, width, fill):
     hidden = hid.shape[1]
     parts = [slice(i * width, (i + 1) * width) for i in range(hidden // width)]
     x = x_ref[...]
@@ -112,25 +114,30 @@
         low[:, c] = (h * gains[0:1, c]).astype(BF16)
         s = jnp.sum(h * h, axis=1, keepdims=True)
         total = s if total is None else total + s
+        fill()
     half = lax.rsqrt(total * (1.0 / hidden) + 1e-6) * 0.5
     for c in parts:
         v = dot(low[...], w_up[:, c]) * half
         act[:, c] = (v + v * jnp.tanh(v)).astype(BF16)
+        fill()
     total = None
     for c in parts:
         h = hid[:, c] + dot(act[...], w_down[:, c])
         low[:, c] = (h * gains[1:2, c]).astype(BF16)
         s = jnp.sum(h * h, axis=1, keepdims=True)
         total = s if total is None else total + s
+        fill()
     scale = lax.rsqrt(total * (1.0 / hidden) + 1e-6)
     return dot(low[...], w_out[...]) * scale
 
 
 def main_kernel(
     sizes, per_peer, rows, capacity, group, width,
-    send_ref, slots_ref, land_ref, gains_ref, w_in_ref, w_up_ref, w_down_ref, w_out_ref,
-    fresh_ref, got_slots, flux_ref,
-    got, slots_s, land, w_in, w_up, w_down, w_out, state, forcing, x, hid, low, act, flux, back,
+    tf_hbm, gap_hbm, lapse_hbm, tile_hbm, target_hbm,
+    land_hbm, gains_hbm, w_in_hbm, w_up_hbm, w_down_hbm, w_out_hbm,
+    fresh_ref, got_slots, flux_ref, hots_ref, counts_ref,
+    tf, gap, lapse, tile, target, land, gains, w_in, w_up, w_down, w_out,
+    send, slots, got, slots_s, ahead_state, state, forcing, x, hid, low, act, flux, back,
     load_sem, slot_send, slot_recv, send_sem, recv_sem, back_send, back_recv, smem_sem,
 ):
     n_atm, n_land = sizes
@@ -160,11 +167,17 @@
         pltpu.make_async_copy(src, dst, load_sem.at[i])
         for i, (src, dst) in enumerate(
             [
-                (land_ref, land.at[pl.ds(0, capacity)]),
-                (w_in_ref, w_in),
-                (w_up_ref, w_up),
-                (w_down_ref, w_down),
-                (w_out_ref, w_out),
+                (target_hbm, target),
+                (tile_hbm, tile),
+                (gap_hbm, gap),
+                (lapse_hbm, lapse),
+                (tf_hbm, tf),
+                (land_hbm, land.at[pl.ds(0, capacity)]),
+                (gains_hbm, gains),
+                (w_in_hbm, w_in),
+                (w_up_hbm, w_up),
+                (w_down_hbm, w_down),
+                (w_out_hbm, w_out),
             ]
         )
     ]
@@ -172,21 +185,26 @@
         load.start()
     land[pl.ds(capacity, 8), :] = jnp.zeros((8, LANES), F32)
     flux[pl.ds(block, 8), :] = jnp.zeros((8, LANES), F32)
-    got_slots[0] = slots_ref[me]
-    got[0] = send_ref[me]
+    for load in loads[:5]:
+        load.wait()
+    prepare(
+        n, per_peer, rows, capacity, tf, gap, lapse, tile, target, send, slots, hots_ref, counts_ref
+    )
+    got_slots[0] = slots[me]
+    got[0] = send[me]
     pl.semaphore_wait(barrier, n - 1)
 
     def slot_copy(d):
         a, b = ahead(d)
         return pltpu.make_async_remote_copy(
-            src_ref=slots_ref.at[a * n_land + b], dst_ref=got_slots.at[d],
+            src_ref=slots.at[a * n_land + b], dst_ref=got_slots.at[d],
             send_sem=slot_send, recv_sem=slot_recv, device_id=(a, b), device_id_type=MESH,
         )
 
     def forcing_copy(d):
         a, b = ahead(d)
         return pltpu.make_async_remote_copy(
-            src_ref=send_ref.at[a * n_land + b], dst_ref=got.at[d],
+            src_ref=send.at[a * n_land + b], dst_ref=got.at[d],
             send_sem=send_sem, recv_sem=recv_sem.at[d // group], device_id=(a, b), device_id_type=MESH,
         )
 
@@ -212,8 +230,19 @@
     to_smem = pltpu.make_async_copy(got_slots, slots_s, smem_sem)
     to_smem.start()
     to_smem.wait()
-    for load in loads:
+    for load in loads[5:]:
         load.wait()
+
+    def fetch(peer, p, k):
+        slot = jnp.clip(slots_s[peer, 0, k], 0, capacity)
+        ahead_state[pl.ds(p * per_peer + k, 1), :] = land[pl.ds(slot, 1), :]
+
+    def fetch_all(p, carry):
+        for k in range(per_peer):
+            fetch(p, p, k)
+        return carry
+
+    lax.fori_loop(0, group, fetch_all, 0)
 
     def chunk(g, carry):
         first = g * group
@@ -227,13 +256,21 @@
             many(got, first, group, send_sem, recv_sem.at[g]).wait_recv()
 
         for p in range(group):
-            for k in range(per_peer):
-                slot = slots_s[first + p, 0, k]
-                state[pl.ds(p * per_peer + k, 1), :] = land[pl.ds(slot, 1), :]
             forcing[pl.ds(p * per_peer, per_peer), :] = got[first + p, :per_peer, :].astype(F32)
         x[:, :LANES] = forcing[...].astype(BF16)
-        x[:, LANES:] = state[...].astype(BF16)
-        result = net(x, hid, low, act, gains_ref, w_in, w_up, w_down, w_out, width)
+        now = ahead_state[...]
+        state[...] = now
+        x[:, LANES:] = now.astype(BF16)
+        following = jnp.minimum(first + group, n - group)
+        todo = [(p, k) for p in range(group) for k in range(per_peer)]
+        share = -(-len(todo) // (3 * (hid.shape[1] // width)))
+
+        def fill():
+            for p, k in todo[:share]:
+                fetch(following + p, p, k)
+            del todo[:share]
+
+        result = net(x, hid, low, act, gains, w_in, w_up, w_down, w_out, width, fill)
         tendency = result[:, :LANES].astype(BF16).astype(F32)
         fresh_ref[pl.ds(pl.multiple_of(g * block, 8), block), :] = state[...] + tendency
         flux[pl.ds(0, block), :] = result[:, LANES:]
@@ -263,25 +300,10 @@
     many(back, 1, n - 1, back_send, back_recv).wait_recv()
 
 
-def finish_kernel(n, per_peer, capacity, slots_ref, fresh_ref, flux_ref, hots_ref, counts_ref,
-                  state_ref, tile_ref, out, sem):
-    def clear(i, carry):
-        out[pl.ds(i * 64, 64), :] = jnp.zeros((64, LANES), F32)
-        return carry
-
-    lax.fori_loop(0, capacity // 64, clear, 0)
-    if capacity % 64:
-        out[pl.ds(capacity // 64 * 64, capacity % 64), :] = jnp.zeros((capacity % 64, LANES), F32)
-
-    def place(d, carry):
-        for k in range(per_peer):
-            slot = slots_ref[d, 0, k]
-            out[pl.ds(slot, 1), :] = fresh_ref[pl.ds(d * per_peer + k, 1), :]
-        return carry
-
-    lax.fori_loop(0, n, place, 0)
-    copy = pltpu.make_async_copy(out.at[pl.ds(0, capacity)], state_ref, sem)
-    copy.start()
+def finish_kernel(n, per_peer, capacity, slots_hbm, fresh_ref, flux_ref, hots_ref, counts_ref,
+                  state_ref, tile_ref, out, slots_ref, sem, smem_sem):
+    to_smem = pltpu.make_async_copy(slots_hbm, slots_ref, smem_sem)
+    to_smem.start()
     total = hots_ref.shape[0]
     step = total // 8
     acc = None
@@ -290,6 +312,25 @@
         t = dot_tn(hots_ref[part, :], flux_ref[part, :])
         acc = t if acc is None else acc + t
     tile_ref[...] = acc / counts_ref[...]
+
+    def clear(i, carry):
+        out[pl.ds(i * 64, 64), :] = jnp.zeros((64, LANES), F32)
+        return carry
+
+    lax.fori_loop(0, capacity // 64, clear, 0)
+    if capacity % 64:
+        out[pl.ds(capacity // 64 * 64, capacity % 64), :] = jnp.zeros((capacity % 64, LANES), F32)
+
+    def place(d, carry):
+        for k in range(per_peer):
+            slot = slots_ref[d, 0, k]
+            out[pl.ds(slot, 1), :] = fresh_ref[pl.ds(d * per_peer + k, 1), :]
+        return carry
+
+    to_smem.wait()
+    lax.fori_loop(0, n, place, 0)
+    copy = pltpu.make_async_copy(out.at[pl.ds(0, capacity)], state_ref, sem)
+    copy.start()
     copy.wait()
 
 
@@ -311,37 +352,32 @@
     group = 16 if n % 16 == 0 else 2
     block = group * per_peer
     S = jax.ShapeDtypeStruct
-    send, slots, hots, counts = pl.pallas_call(
-        functools.partial(prep_kernel, n, per_peer, rows, capacity),
-        out_shape=[
-            S((n, rows, features), BF16), S((n, LANES), jnp.int32),
-            S((n, rows, tiles), BF16), S((tiles, features), F32),
-        ],
-        in_specs=[VMEM] * 5,
-        out_specs=[VMEM] * 4,
-        compiler_params=limit(48),
-        name="prep",
-    )(
-        tile_forcing, elevation_gap.reshape(1, columns), lapse_rate.reshape(1, features),
-        column_tile.reshape(1, columns), column_target.reshape(1, columns),
-    )
-    slots = slots.reshape(n, 1, LANES)
     dma = pltpu.SemaphoreType.DMA
-    fresh, got_slots, flux = pl.pallas_call(
+    fresh, got_slots, flux, hots, counts = pl.pallas_call(
         functools.partial(main_kernel, sizes, per_peer, rows, capacity, group, 256),
         out_shape=[
             S((n * per_peer, features), F32), S((n, 1, LANES), jnp.int32), S((n, rows, features), BF16),
+            S((n, rows, tiles), BF16), S((tiles, features), F32),
         ],
-        in_specs=[VMEM, VMEM, ANY, VMEM, ANY, ANY, ANY, ANY],
-        out_specs=[VMEM] * 3,
+        in_specs=[HBM] * 11,
+        out_specs=[VMEM] * 5,
         scratch_shapes=[
-            pltpu.VMEM((n, rows, features), BF16),
-            pltpu.SMEM((n, 1, LANES), jnp.int32),
+            pltpu.VMEM((tiles, features), BF16),
+            pltpu.VMEM((1, columns), F32),
+            pltpu.VMEM((1, features), F32),
+            pltpu.VMEM((1, columns), jnp.int32),
+            pltpu.VMEM((1, columns), jnp.int32),
             pltpu.VMEM((capacity + 8, features), F32),
+            pltpu.VMEM(norm_gains.shape, F32),
             pltpu.VMEM(w_in.shape, BF16),
             pltpu.VMEM(w_up.shape[1:], BF16),
             pltpu.VMEM(w_down.shape[1:], BF16),
             pltpu.VMEM(w_out.shape, BF16),
+            pltpu.VMEM((n, rows, features), BF16),
+            pltpu.VMEM((n, 1, LANES), jnp.int32),
+            pltpu.VMEM((n, rows, features), BF16),
+            pltpu.SMEM((n, 1, LANES), jnp.int32),
+            pltpu.VMEM((block, features), F32),
             pltpu.VMEM((block, features), F32),
             pltpu.VMEM((block, features), F32),
             pltpu.VMEM((block, 2 * features), BF16),
@@ -350,20 +386,32 @@
             pltpu.VMEM((block, hidden), BF16),
             pltpu.VMEM((block + 8, features), F32),
             pltpu.VMEM((n, rows, features), BF16),
-            dma((5,)), dma(()), dma(()), dma(()), dma((n // group,)), dma(()), dma(()), dma(()),
+            dma((11,)), dma(()), dma(()), dma(()), dma((n // group,)), dma(()), dma(()), dma(()),
         ],
         compiler_params=pltpu.CompilerParams(
-            collective_id=0, has_side_effects=True, vmem_limit_bytes=60 * 1024 * 1024
+            collective_id=0, has_side_effects=True, vmem_limit_bytes=40 * 1024 * 1024
         ),
         name="exchange",
-    )(send, slots, land_state, norm_gains, w_in, w_up[0], w_down[0], w_out)
+    )(
+        *[
+            pltpu.with_memory_space_constraint(v, pltpu.HBM)
+            for v in (
+                tile_forcing, elevation_gap.reshape(1, columns), lapse_rate.reshape(1, features),
+                column_tile.reshape(1, columns), column_target.reshape(1, columns),
+                land_state, norm_gains, w_in, w_up[0], w_down[0], w_out,
+            )
+        ]
+    )
     return pl.pallas_call(
         functools.partial(finish_kernel, n, per_peer, capacity),
         out_shape=[S((capacity, features), F32), S((tiles, features), F32)],
-        in_specs=[SMEM, VMEM, VMEM, VMEM, VMEM],
+        in_specs=[VMEM] * 5,
         out_specs=[ANY, VMEM],
-        scratch_shapes=[pltpu.VMEM((capacity + 8, features), F32), dma(())],
-        compiler_params=limit(32),
+        scratch_shapes=[
+            pltpu.VMEM((capacity + 8, features), F32), pltpu.SMEM((n, 1, LANES), jnp.int32),
+            dma(()), dma(()),
+        ],
+        compiler_params=limit(24),
         name="finish",
     )(
         got_slots, fresh, flux.reshape(n * rows, features), hots.reshape(n * rows, tiles), counts

time: 94.5 us -> 78.8 us (0.83)
  the two profiles are of different devices: /device:TPU:1 before, /device:TPU:33 now
where the time goes in v2:
time: 78.8 us; the launch traced here: 78.6 us
  Pallas kernels  78 us (99%)
    pallas_call x1, Pallas kernels, local(): pl.pallas_call(functools.partial(main_kernel, sizes, per_peer, rows, capa...  69 us
    pallas_call x1, Pallas kernels, local(): pl.pallas_call(functools.partial(finish_kernel, n, per_peer, capacity), o...  8.97 us

profile of v2, /device:TPU:33, one launch (start us, length us, event | category | flops | bytes accessed | tf_op | source)
XLA Modules:
  0.0 78.6 jit_solution(1908533065528877534)
XLA Ops:
  0.6 69.0 %exchange.1 = (f32[5248,128]{1,0:T(8,128)S(1)}, s32[128,1,128]{2,1,0:T(1,128)S(1)}, bf16[128,48,128]{2,1,0:T(8,128)(2,1)S(1)}, bf16[128,48,128]{2,1,0:T(8,128)(2,1)S(1)}, f32[128,128]{1,0:T(8,128)S(1)}) custom-call(bf16[128,128]{1,0:T(8,128)(2,1)} %tf_hbm.1, f32[1,2048]{1,0:T(1,128)} %bitcast.12, f32[1,128]{1,0:T(1,128)} %bitcast.15, s32[1,2048]{1,0:T(1,128)} %bitcast.13, ...), custom_call_target="tpu_custom_call" | custom-call | tf_op jit(solution)/shard_map/exchange/pallas_call | solution.py:356
  69.7 9.0 %finish.1 = (f32[5120,128]{1,0:T(8,128)}, f32[128,128]{1,0:T(8,128)}) custom-call(s32[128,1,128]{2,1,0:T(1,128)S(1)} %get-tuple-element.7.slots_hbm, f32[5248,128]{1,0:T(8,128)S(1)} %get-tuple-element.8.fresh_ref, bf16[6144,128]{1,0:T(8,128)(2,1)S(1)} %bitcast.8, bf16[6144,128]{1,0:T(8,128)(2,1)S(1)} %bitcast.9, f32[128,128]{1,0:T(8,128)S(1)} %get-tuple-element.11.counts_ref), custom_call_target="tpu_custom_call" | custom-call | tf_op jit(solution)/shard_map/finish/pallas_call | solution.py:405

commit v3 on v2

--- a/solution.py
+++ b/solution.py
@@ -10,6 +10,7 @@
 F32 = jnp.float32
 BF16 = jnp.bfloat16
 LANES = 128
+HALF = 64
 VMEM = pl.BlockSpec(memory_space=pltpu.VMEM)
 HBM = pl.BlockSpec(memory_space=pltpu.HBM)
 ANY = pl.BlockSpec(memory_space=pl.ANY)
@@ -36,17 +37,22 @@
     return jnp.where(mask, 1.0, 0.0)
 
 
-def prepare(
-    n, per_peer, rows, capacity, tf_ref, gap_ref, lapse_ref, tile_ref, target_ref,
-    send_ref, slots_ref, hots_ref, counts_ref,
-):
+def tables(sizes, atm, lnd, per_peer, rows, capacity, gap_ref, tile_ref, target_ref, counts_ref):
+    n_atm, n_land = sizes
+    n = n_atm * n_land
     columns = target_ref.shape[1]
-    tiles = tf_ref.shape[0]
+    tiles = counts_ref.shape[0]
     target = target_ref[...].astype(F32)
     owner_f = jnp.floor((target + 0.5) * (1.0 / capacity))
     slot_p = target - owner_f * capacity + 1.0
-    owner = owner_f.astype(jnp.int32)
-    owner_hot = hot(iota((n, columns), 0) == owner)
+    owner_atm = jnp.floor((owner_f + 0.5) * (1.0 / n_land))
+    owner_land = owner_f - owner_atm * n_land
+    step = owner_land - lnd.astype(F32)
+    step = jnp.where(step < 0.0, step + n_land, step)
+    turn = owner_atm - atm.astype(F32) - step + (n_land + n_atm)
+    turn = turn - jnp.floor((turn + 0.5) * (1.0 / n_atm)) * n_atm
+    order = (turn * n_land + step).astype(jnp.int32)
+    owner_hot = hot(iota((n, columns), 0) == order)
     owner_bf = owner_hot.astype(BF16)
     block = min(256, columns)
     upper = hot(iota((block, block), 0) <= iota((block, block), 1)).astype(BF16)
@@ -58,15 +64,11 @@
         ranks.append(jnp.sum(owner_hot[:, part] * (seen + running), axis=0, keepdims=True) - 1.0)
         running = running + seen[:, block - 1 : block]
     rank = jnp.concatenate(ranks, axis=1).astype(jnp.int32)
-    place = hot(iota((LANES, columns), 0) == rank)
+    place = hot(iota((HALF, columns), 0) == rank)
     high = jnp.floor(slot_p * (1.0 / 64.0))
     low = slot_p - 64.0 * high
-    slot_hi = dot_nt(owner_bf, (place * high).astype(BF16))
-    slot_lo = dot_nt(owner_bf, (place * low).astype(BF16))
-    slot = slot_hi * 64.0 + slot_lo - 1.0
-    slot = jnp.where(slot < 0.0, float(capacity), slot).astype(jnp.int32)
-    for j in range(n):
-        slots_ref[j] = slot[j : j + 1, :]
+    both = jnp.concatenate([(place * high).astype(BF16), (place * low).astype(BF16)], axis=0)
+    slot_rows = dot_nt(owner_bf, both)
     tile = tile_ref[...]
     gap = gap_ref[...]
     gap_1 = gap.astype(BF16).astype(F32)
@@ -80,27 +82,7 @@
     ) + dot_nt((short * gap_3).astype(BF16), owner_bf)
     number = jnp.sum(hot(iota((tiles, columns), 0) == tile), axis=1, keepdims=True)
     counts_ref[...] = jnp.broadcast_to(jnp.maximum(number, 1.0), counts_ref.shape)
-    group = min(16, n)
-    lapse = lapse_ref[...]
-    table = tf_ref[...]
-    lane = iota((rows, tiles), 1).astype(F32) + 1.0
-
-    def body(b, carry):
-        tile_now, gap_now = carry
-        hots = jnp.concatenate(
-            [hot(lane == tile_now[:, i : i + 1]).astype(BF16) for i in range(group)], axis=0
-        )
-        lifts = jnp.concatenate([gap_now[:, i : i + 1] * lapse for i in range(group)], axis=0)
-        forcing = (dot(hots, table) + lifts).astype(BF16)
-        spot = pl.ds(b * group, group)
-        hots_ref[spot] = hots.reshape(group, rows, tiles)
-        send_ref[spot] = forcing.reshape(group, rows, LANES)
-        return (
-            pltpu.roll(tile_now, n - group, axis=1) if n > group else tile_now,
-            pltpu.roll(gap_now, n - group, axis=1) if n > group else gap_now,
-        )
-
-    lax.fori_loop(0, n // group, body, (tile_of, gap_of))
+    return slot_rows, tile_of, gap_of
 
 
 def net(x_ref, hid, low, act, gains, w_in, w_up, w_down, w_out, width, fill):
@@ -132,37 +114,48 @@
 
 
 def main_kernel(
-    sizes, per_peer, rows, capacity, group, width,
+    sizes, per_peer, rows, capacity, width,
     tf_hbm, gap_hbm, lapse_hbm, tile_hbm, target_hbm,
     land_hbm, gains_hbm, w_in_hbm, w_up_hbm, w_down_hbm, w_out_hbm,
     fresh_ref, got_slots, flux_ref, hots_ref, counts_ref,
     tf, gap, lapse, tile, target, land, gains, w_in, w_up, w_down, w_out,
-    send, slots, got, slots_s, ahead_state, state, forcing, x, hid, low, act, flux, back,
-    load_sem, slot_send, slot_recv, send_sem, recv_sem, back_send, back_recv, smem_sem,
+    send, slot_rows, tile_of, gap_of, got, slots_s, ahead_state, state, forcing, x, hid, low, act,
+    flux, back, load_sem, send_sem, recv_sem, back_send, back_recv, smem_sem,
 ):
     n_atm, n_land = sizes
     n = n_atm * n_land
+    group = n_land
+    tiles = tf.shape[0]
     atm = lax.axis_index("atm")
     lnd = lax.axis_index("land")
-    me = atm * n_land + lnd
     block = group * per_peer
-
-    def ahead(d):
-        return lax.rem(atm + d // n_land, n_atm), lax.rem(lnd + lax.rem(d, n_land), n_land)
-
-    def behind(d):
-        return (
-            lax.rem(atm - d // n_land + n_atm, n_atm),
-            lax.rem(lnd - lax.rem(d, n_land) + n_land, n_land),
-        )
+    last = n_atm - 1
+    message = pl.ds(0, -(-(per_peer + 1) // 2) * 2)
+
+    def atm_ahead(g, p):
+        return lax.rem(atm + g + p, n_atm)
+
+    def atm_behind(g, p):
+        return lax.rem(atm - g - p + n_atm + n_land + n_atm, n_atm)
+
+    lands_ahead = [lax.rem(lnd + p, n_land) for p in range(n_land)]
+    lands_behind = [lax.rem(lnd - p + n_land, n_land) for p in range(n_land)]
 
     barrier = pltpu.get_barrier_semaphore()
 
-    def greet(d, carry):
-        pl.semaphore_signal(barrier, inc=1, device_id=ahead(d), device_id_type=MESH)
-        return carry
-
-    lax.fori_loop(1, n, greet, 0)
+    def greet(g, carry):
+        for p in range(group):
+            def hello():
+                pl.semaphore_signal(
+                    barrier, inc=1, device_id=(atm_ahead(g, p), lands_ahead[p]), device_id_type=MESH
+                )
+
+            if p == 0:
+                pl.when(g > 0)(hello)
+            else:
+                hello()
+        return carry
+
     loads = [
         pltpu.make_async_copy(src, dst, load_sem.at[i])
         for i, (src, dst) in enumerate(
@@ -183,55 +176,87 @@
     ]
     for load in loads:
         load.start()
+    spare = rows - 16
+    flux_ref[:, spare:, :] = jnp.zeros((n, 16, LANES), BF16)
+    lax.fori_loop(0, n_atm, greet, 0)
     land[pl.ds(capacity, 8), :] = jnp.zeros((8, LANES), F32)
     flux[pl.ds(block, 8), :] = jnp.zeros((8, LANES), F32)
     for load in loads[:5]:
         load.wait()
-    prepare(
-        n, per_peer, rows, capacity, tf, gap, lapse, tile, target, send, slots, hots_ref, counts_ref
+    slot_rows[...], tile_of[...], gap_of[...] = tables(
+        sizes, atm, lnd, per_peer, rows, capacity, gap, tile, target, counts_ref
     )
-    got_slots[0] = slots[me]
-    got[0] = send[me]
+    lane = iota((rows, tiles), 1).astype(F32) + 1.0
+    last_row = hot(iota((rows, LANES), 0) == per_peer)
+
+    def build(g):
+        base = g * group
+        turn = lax.rem(n - base, n)
+        tile_now = pltpu.roll(tile_of[...], turn, axis=1)
+        gap_now = pltpu.roll(gap_of[...], turn, axis=1)
+        slot_now = slot_rows[pl.ds(pl.multiple_of(base, group), group), :]
+        hots = jnp.concatenate(
+            [hot(lane == tile_now[:, i : i + 1]).astype(BF16) for i in range(group)], axis=0
+        )
+        extra = jnp.concatenate(
+            [
+                gap_now[:, i : i + 1] * lapse[...] + last_row * slot_now[i : i + 1, :]
+                for i in range(group)
+            ],
+            axis=0,
+        )
+        made = (dot(hots, tf[...]) + extra).astype(BF16)
+        spot = pl.ds(base, group)
+        hots_ref[spot] = hots.reshape(group, rows, tiles)
+        send[spot] = made.reshape(group, rows, LANES)
+
+    def dispatch(g):
+        for p in range(group):
+            def go():
+                pltpu.make_async_remote_copy(
+                    src_ref=send.at[g * group + p, message],
+                    dst_ref=got.at[g * group + p, message],
+                    send_sem=send_sem, recv_sem=recv_sem.at[g],
+                    device_id=(atm_ahead(g, p), lands_ahead[p]), device_id_type=MESH,
+                ).start()
+
+            if p == 0:
+                pl.when(g > 0)(go)
+            else:
+                go()
+
+    build(0)
+    got[0] = send[0]
     pl.semaphore_wait(barrier, n - 1)
 
-    def slot_copy(d):
-        a, b = ahead(d)
+    def build_and_send(g, carry):
+        build(g)
+        dispatch(g - 1)
+        return carry
+
+    lax.fori_loop(1, n_atm, build_and_send, 0)
+    dispatch(last)
+
+    def many(ref, start, count, sending, receiving):
+        spot = ref.at[pl.ds(start, count), message]
         return pltpu.make_async_remote_copy(
-            src_ref=slots.at[a * n_land + b], dst_ref=got_slots.at[d],
-            send_sem=slot_send, recv_sem=slot_recv, device_id=(a, b), device_id_type=MESH,
+            src_ref=spot, dst_ref=spot, send_sem=sending, recv_sem=receiving,
+            device_id=(atm, lands_ahead[1]), device_id_type=MESH,
         )
 
-    def forcing_copy(d):
-        a, b = ahead(d)
-        return pltpu.make_async_remote_copy(
-            src_ref=send.at[a * n_land + b], dst_ref=got.at[d],
-            send_sem=send_sem, recv_sem=recv_sem.at[d // group], device_id=(a, b), device_id_type=MESH,
-        )
-
-    def start_slots(d, carry):
-        slot_copy(d).start()
-        return carry
-
-    def start_forcing(d, carry):
-        forcing_copy(d).start()
-        return carry
-
-    lax.fori_loop(1, n, start_slots, 0)
-    lax.fori_loop(1, n, start_forcing, 0)
-
-    def many(ref, start, count, send, recv):
-        spot = ref.at[pl.ds(start, count)]
-        return pltpu.make_async_remote_copy(
-            src_ref=spot, dst_ref=spot, send_sem=send, recv_sem=recv,
-            device_id=ahead(1), device_id_type=MESH,
-        )
-
-    many(got_slots, 1, n - 1, slot_send, slot_recv).wait_recv()
-    to_smem = pltpu.make_async_copy(got_slots, slots_s, smem_sem)
-    to_smem.start()
-    to_smem.wait()
-    for load in loads[5:]:
-        load.wait()
+    def to_smem(g):
+        spot = pl.ds(g * group, group)
+        return pltpu.make_async_copy(got_slots.at[spot], slots_s.at[spot], smem_sem.at[lax.rem(g, 2)])
+
+    base_row = per_peer // 16 * 16
+
+    def decode(g):
+        for p in range(group):
+            tail = got[g * group + p, pl.ds(base_row, 16), :].astype(F32)
+            row = tail[per_peer - base_row : per_peer - base_row + 1, :]
+            slot = row * 64.0 + pltpu.roll(row, HALF, axis=1) - 1.0
+            got_slots[g * group + p] = jnp.where(slot < 0.0, float(capacity), slot).astype(jnp.int32)
+        to_smem(g).start()
 
     def fetch(peer, p, k):
         slot = jnp.clip(slots_s[peer, 0, k], 0, capacity)
@@ -242,18 +267,27 @@
             fetch(p, p, k)
         return carry
 
+    many(got, 1, group - 1, send_sem, recv_sem.at[0]).wait_recv()
+    decode(0)
+    for load in loads[5:]:
+        load.wait()
+    to_smem(0).wait()
     lax.fori_loop(0, group, fetch_all, 0)
+    if last > 0:
+        many(got, group, group, send_sem, recv_sem.at[1]).wait_recv()
+        decode(1)
 
     def chunk(g, carry):
         first = g * group
 
-        @pl.when(g == 0)
+        @pl.when(g < last - 1)
         def _():
-            many(got, 1, group - 1, send_sem, recv_sem.at[0]).wait_recv()
-
-        @pl.when(g > 0)
+            many(got, first + 2 * group, group, send_sem, recv_sem.at[g + 2]).wait_recv()
+            decode(g + 2)
+
+        @pl.when(g < last)
         def _():
-            many(got, first, group, send_sem, recv_sem.at[g]).wait_recv()
+            to_smem(g + 1).wait()
 
         for p in range(group):
             forcing[pl.ds(p * per_peer, per_peer), :] = got[first + p, :per_peer, :].astype(F32)
@@ -276,25 +310,23 @@
         flux[pl.ds(0, block), :] = result[:, LANES:]
         for p in range(group):
             back[first + p] = flux[pl.ds(p * per_peer, rows), :].astype(BF16)
-
-        def give(p, carry):
-            d = first + p
-
-            @pl.when(d > 0)
-            def _():
+        for p in range(group):
+            def give():
+                a = atm_behind(g, p)
                 pltpu.make_async_remote_copy(
-                    src_ref=back.at[d], dst_ref=flux_ref.at[me],
-                    send_sem=back_send, recv_sem=back_recv, device_id=behind(d), device_id_type=MESH,
+                    src_ref=back.at[first + p, message], dst_ref=flux_ref.at[first + p, message],
+                    send_sem=back_send, recv_sem=back_recv,
+                    device_id=(a, lands_behind[p]), device_id_type=MESH,
                 ).start()
 
-            return carry
-
-        lax.fori_loop(0, group, give, 0)
-        return carry
-
-    lax.fori_loop(0, n // group, chunk, 0)
-    flux_ref[me] = back[0]
-    many(got_slots, 1, n - 1, slot_send, slot_recv).wait_send()
+            if p == 0:
+                pl.when(g > 0)(give)
+            else:
+                give()
+        return carry
+
+    lax.fori_loop(0, n_atm, chunk, 0)
+    flux_ref[0] = back[0]
     many(got, 1, n - 1, send_sem, recv_sem.at[0]).wait_send()
     many(back, 1, n - 1, back_send, back_recv).wait_send()
     many(back, 1, n - 1, back_send, back_recv).wait_recv()
@@ -302,8 +334,16 @@
 
 def finish_kernel(n, per_peer, capacity, slots_hbm, fresh_ref, flux_ref, hots_ref, counts_ref,
                   state_ref, tile_ref, out, slots_ref, sem, smem_sem):
-    to_smem = pltpu.make_async_copy(slots_hbm, slots_ref, smem_sem)
-    to_smem.start()
+    parts = 4
+    span = n // parts
+    copies = [
+        pltpu.make_async_copy(
+            slots_hbm.at[pl.ds(i * span, span)], slots_ref.at[pl.ds(i * span, span)], smem_sem.at[i]
+        )
+        for i in range(parts)
+    ]
+    for copy in copies:
+        copy.start()
     total = hots_ref.shape[0]
     step = total // 8
     acc = None
@@ -327,8 +367,9 @@
             out[pl.ds(slot, 1), :] = fresh_ref[pl.ds(d * per_peer + k, 1), :]
         return carry
 
-    to_smem.wait()
-    lax.fori_loop(0, n, place, 0)
+    for i in range(parts):
+        copies[i].wait()
+        lax.fori_loop(i * span, (i + 1) * span, place, 0)
     copy = pltpu.make_async_copy(out.at[pl.ds(0, capacity)], state_ref, sem)
     copy.start()
     copy.wait()
@@ -349,12 +390,12 @@
     columns = elevation_gap.shape[0]
     tiles, features = tile_forcing.shape
     hidden = w_in.shape[1]
-    group = 16 if n % 16 == 0 else 2
+    group = sizes[1]
     block = group * per_peer
     S = jax.ShapeDtypeStruct
     dma = pltpu.SemaphoreType.DMA
     fresh, got_slots, flux, hots, counts = pl.pallas_call(
-        functools.partial(main_kernel, sizes, per_peer, rows, capacity, group, 256),
+        functools.partial(main_kernel, sizes, per_peer, rows, capacity, 256),
         out_shape=[
             S((n * per_peer, features), F32), S((n, 1, LANES), jnp.int32), S((n, rows, features), BF16),
             S((n, rows, tiles), BF16), S((tiles, features), F32),
@@ -374,7 +415,9 @@
             pltpu.VMEM(w_down.shape[1:], BF16),
             pltpu.VMEM(w_out.shape, BF16),
             pltpu.VMEM((n, rows, features), BF16),
-            pltpu.VMEM((n, 1, LANES), jnp.int32),
+            pltpu.VMEM((n, LANES), F32),
+            pltpu.VMEM((rows, n), F32),
+            pltpu.VMEM((rows, n), F32),
             pltpu.VMEM((n, rows, features), BF16),
             pltpu.SMEM((n, 1, LANES), jnp.int32),
             pltpu.VMEM((block, features), F32),
@@ -386,7 +429,7 @@
             pltpu.VMEM((block, hidden), BF16),
             pltpu.VMEM((block + 8, features), F32),
             pltpu.VMEM((n, rows, features), BF16),
-            dma((11,)), dma(()), dma(()), dma(()), dma((n // group,)), dma(()), dma(()), dma(()),
+            dma((11,)), dma(()), dma((n // group,)), dma(()), dma(()), dma((2,)),
         ],
         compiler_params=pltpu.CompilerParams(
             collective_id=0, has_side_effects=True, vmem_limit_bytes=40 * 1024 * 1024
@@ -409,7 +452,7 @@
         out_specs=[ANY, VMEM],
         scratch_shapes=[
             pltpu.VMEM((capacity + 8, features), F32), pltpu.SMEM((n, 1, LANES), jnp.int32),
-            dma(()), dma(()),
+            dma(()), dma((4,)),
         ],
         compiler_params=limit(24),
         name="finish",

time: 78.8 us -> 70.9 us (0.90)
  the two profiles are of different devices: /device:TPU:33 before, /device:TPU:1 now
where the time goes in v3:
time: 70.9 us; the launch traced here: 70.8 us
  Pallas kernels  70.2 us (99%)
    pallas_call x1, Pallas kernels, local(): pl.pallas_call(functools.partial(main_kernel, sizes, per_peer, rows, capa...  62 us
    pallas_call x1, Pallas kernels, local(): pl.pallas_call(functools.partial(finish_kernel, n, per_peer, capacity), o...  8.16 us

profile of v3, /device:TPU:1, one launch (start us, length us, event | category | flops | bytes accessed | tf_op | source)
XLA Modules:
  0.0 70.8 jit_solution(7325583790426910018)
XLA Ops:
  0.6 62.0 %exchange.1 = (f32[5248,128]{1,0:T(8,128)S(1)}, s32[128,1,128]{2,1,0:T(1,128)S(1)}, bf16[128,48,128]{2,1,0:T(8,128)(2,1)S(1)}, bf16[128,48,128]{2,1,0:T(8,128)(2,1)S(1)}, f32[128,128]{1,0:T(8,128)S(1)}) custom-call(bf16[128,128]{1,0:T(8,128)(2,1)} %tf_hbm.1, f32[1,2048]{1,0:T(1,128)} %bitcast.12, f32[1,128]{1,0:T(1,128)} %bitcast.15, s32[1,2048]{1,0:T(1,128)} %bitcast.13, ...), custom_call_target="tpu_custom_call" | custom-call | tf_op jit(solution)/shard_map/exchange/pallas_call | solution.py:397
  62.6 8.2 %finish.1 = (f32[5120,128]{1,0:T(8,128)}, f32[128,128]{1,0:T(8,128)}) custom-call(s32[128,1,128]{2,1,0:T(1,128)S(1)} %get-tuple-element.7.slots_hbm, f32[5248,128]{1,0:T(8,128)S(1)} %get-tuple-element.8.fresh_ref, bf16[6144,128]{1,0:T(8,128)(2,1)S(1)} %bitcast.8, bf16[6144,128]{1,0:T(8,128)(2,1)S(1)} %bitcast.9, f32[128,128]{1,0:T(8,128)S(1)} %get-tuple-element.11.counts_ref), custom_call_target="tpu_custom_call" | custom-call | tf_op jit(solution)/shard_map/finish/pallas_call | solution.py:448

commit v4 on v3

--- a/solution.py
+++ b/solution.py
@@ -37,11 +37,10 @@
     return jnp.where(mask, 1.0, 0.0)
 
 
-def tables(sizes, atm, lnd, per_peer, rows, capacity, gap_ref, tile_ref, target_ref, counts_ref):
+def tables(sizes, atm, lnd, per_peer, rows, capacity, gap_ref, tile_ref, target_ref):
     n_atm, n_land = sizes
     n = n_atm * n_land
     columns = target_ref.shape[1]
-    tiles = counts_ref.shape[0]
     target = target_ref[...].astype(F32)
     owner_f = jnp.floor((target + 0.5) * (1.0 / capacity))
     slot_p = target - owner_f * capacity + 1.0
@@ -80,8 +79,6 @@
         dot_nt((short * gap_1).astype(BF16), owner_bf)
         + dot_nt((short * gap_2).astype(BF16), owner_bf)
     ) + dot_nt((short * gap_3).astype(BF16), owner_bf)
-    number = jnp.sum(hot(iota((tiles, columns), 0) == tile), axis=1, keepdims=True)
-    counts_ref[...] = jnp.broadcast_to(jnp.maximum(number, 1.0), counts_ref.shape)
     return slot_rows, tile_of, gap_of
 
 
@@ -184,7 +181,7 @@
     for load in loads[:5]:
         load.wait()
     slot_rows[...], tile_of[...], gap_of[...] = tables(
-        sizes, atm, lnd, per_peer, rows, capacity, gap, tile, target, counts_ref
+        sizes, atm, lnd, per_peer, rows, capacity, gap, tile, target
     )
     lane = iota((rows, tiles), 1).astype(F32) + 1.0
     last_row = hot(iota((rows, LANES), 0) == per_peer)
@@ -225,17 +222,19 @@
             else:
                 go()
 
-    build(0)
+    def loop(step):
+        def body(g, carry):
+            step(g)
+            return carry
+
+        lax.fori_loop(0, n_atm, body, 0)
+
+    loop(build)
     got[0] = send[0]
     pl.semaphore_wait(barrier, n - 1)
-
-    def build_and_send(g, carry):
-        build(g)
-        dispatch(g - 1)
-        return carry
-
-    lax.fori_loop(1, n_atm, build_and_send, 0)
-    dispatch(last)
+    loop(dispatch)
+    number = jnp.sum(hot(iota((tiles, tile.shape[1]), 0) == tile[...]), axis=1, keepdims=True)
+    counts_ref[...] = jnp.broadcast_to(jnp.maximum(number, 1.0), counts_ref.shape)
 
     def many(ref, start, count, sending, receiving):
         spot = ref.at[pl.ds(start, count), message]
@@ -280,7 +279,7 @@
     def chunk(g, carry):
         first = g * group
 
-        @pl.when(g < last - 1)
+        @pl.when((g > 0) & (g < last - 1))
         def _():
             many(got, first + 2 * group, group, send_sem, recv_sem.at[g + 2]).wait_recv()
             decode(g + 2)
@@ -323,6 +322,14 @@
                 pl.when(g > 0)(give)
             else:
                 give()
+
+        if last > 1:
+
+            @pl.when(g == 0)
+            def _():
+                many(got, 2 * group, group, send_sem, recv_sem.at[2]).wait_recv()
+                decode(2)
+
         return carry
 
     lax.fori_loop(0, n_atm, chunk, 0)
@@ -336,6 +343,7 @@
                   state_ref, tile_ref, out, slots_ref, sem, smem_sem):
     parts = 4
     span = n // parts
+    unroll = min(8, span)
     copies = [
         pltpu.make_async_copy(
             slots_hbm.at[pl.ds(i * span, span)], slots_ref.at[pl.ds(i * span, span)], smem_sem.at[i]
@@ -361,15 +369,17 @@
     if capacity % 64:
         out[pl.ds(capacity // 64 * 64, capacity % 64), :] = jnp.zeros((capacity % 64, LANES), F32)
 
-    def place(d, carry):
-        for k in range(per_peer):
-            slot = slots_ref[d, 0, k]
-            out[pl.ds(slot, 1), :] = fresh_ref[pl.ds(d * per_peer + k, 1), :]
+    def place(i, carry):
+        for u in range(unroll):
+            d = i * unroll + u
+            for k in range(per_peer):
+                slot = slots_ref[d, 0, k]
+                out[pl.ds(slot, 1), :] = fresh_ref[pl.ds(d * per_peer + k, 1), :]
         return carry
 
     for i in range(parts):
         copies[i].wait()
-        lax.fori_loop(i * span, (i + 1) * span, place, 0)
+        lax.fori_loop(i * span // unroll, (i + 1) * span // unroll, place, 0)
     copy = pltpu.make_async_copy(out.at[pl.ds(0, capacity)], state_ref, sem)
     copy.start()
     copy.wait()
@@ -395,7 +405,7 @@
     S = jax.ShapeDtypeStruct
     dma = pltpu.SemaphoreType.DMA
     fresh, got_slots, flux, hots, counts = pl.pallas_call(
-        functools.partial(main_kernel, sizes, per_peer, rows, capacity, 256),
+        functools.partial(main_kernel, sizes, per_peer, rows, capacity, min(hidden, 1024)),
         out_shape=[
             S((n * per_peer, features), F32), S((n, 1, LANES), jnp.int32), S((n, rows, features), BF16),
             S((n, rows, tiles), BF16), S((tiles, features), F32),

time: 70.9 us -> 70.2 us (level)
  Pallas kernels: 70.2 us -> 69.4 us
where the time goes in v4:
time: 70.2 us; the launch traced here: 70 us
  Pallas kernels  69.4 us (99%)
    pallas_call x1, Pallas kernels, local(): pl.pallas_call(functools.partial(main_kernel, sizes, per_peer, rows, capa...  61.8 us
    pallas_call x1, Pallas kernels, local(): pl.pallas_call(functools.partial(finish_kernel, n, per_peer, capacity), o...  7.64 us

profile of v4, /device:TPU:1, one launch (start us, length us, event | category | flops | bytes accessed | tf_op | source)
XLA Modules:
  0.0 70.0 jit_solution(1946078757081903431)
XLA Ops:
  0.6 61.8 %exchange.1 = (f32[5248,128]{1,0:T(8,128)S(1)}, s32[128,1,128]{2,1,0:T(1,128)S(1)}, bf16[128,48,128]{2,1,0:T(8,128)(2,1)S(1)}, bf16[128,48,128]{2,1,0:T(8,128)(2,1)S(1)}, f32[128,128]{1,0:T(8,128)S(1)}) custom-call(bf16[128,128]{1,0:T(8,128)(2,1)} %tf_hbm.1, f32[1,2048]{1,0:T(1,128)} %bitcast.12, f32[1,128]{1,0:T(1,128)} %bitcast.15, s32[1,2048]{1,0:T(1,128)} %bitcast.13, ...), custom_call_target="tpu_custom_call" | custom-call | tf_op jit(solution)/shard_map/exchange/pallas_call | solution.py:407
  62.4 7.6 %finish.1 = (f32[5120,128]{1,0:T(8,128)}, f32[128,128]{1,0:T(8,128)}) custom-call(s32[128,1,128]{2,1,0:T(1,128)S(1)} %get-tuple-element.7.slots_hbm, f32[5248,128]{1,0:T(8,128)S(1)} %get-tuple-element.8.fresh_ref, bf16[6144,128]{1,0:T(8,128)(2,1)S(1)} %bitcast.8, bf16[6144,128]{1,0:T(8,128)(2,1)S(1)} %bitcast.9, f32[128,128]{1,0:T(8,128)S(1)} %get-tuple-element.11.counts_ref), custom_call_target="tpu_custom_call" | custom-call | tf_op jit(solution)/shard_map/finish/pallas_call | solution.py:458

commit v5 on v4

--- a/solution.py
+++ b/solution.py
@@ -48,7 +48,7 @@
     owner_land = owner_f - owner_atm * n_land
     step = owner_land - lnd.astype(F32)
     step = jnp.where(step < 0.0, step + n_land, step)
-    turn = owner_atm - atm.astype(F32) - step + (n_land + n_atm)
+    turn = owner_atm - atm.astype(F32) - 3.0 * step + (3 * n_land + n_atm)
     turn = turn - jnp.floor((turn + 0.5) * (1.0 / n_atm)) * n_atm
     order = (turn * n_land + step).astype(jnp.int32)
     owner_hot = hot(iota((n, columns), 0) == order)
@@ -130,10 +130,10 @@
     message = pl.ds(0, -(-(per_peer + 1) // 2) * 2)
 
     def atm_ahead(g, p):
-        return lax.rem(atm + g + p, n_atm)
+        return lax.rem(atm + g + 3 * p, n_atm)
 
     def atm_behind(g, p):
-        return lax.rem(atm - g - p + n_atm + n_land + n_atm, n_atm)
+        return lax.rem(atm - g - 3 * p + n_atm + 3 * n_land + n_atm, n_atm)
 
     lands_ahead = [lax.rem(lnd + p, n_land) for p in range(n_land)]
     lands_behind = [lax.rem(lnd - p + n_land, n_land) for p in range(n_land)]

time: 70.2 us -> 69.7 us (level)
  no operation moved by 1% of the time
where the time goes in v5:
time: 69.7 us; the launch traced here: 69.5 us
  Pallas kernels  68.9 us (99%)
    pallas_call x1, Pallas kernels, local(): pl.pallas_call(functools.partial(main_kernel, sizes, per_peer, rows, capa...  61.3 us
    pallas_call x1, Pallas kernels, local(): pl.pallas_call(functools.partial(finish_kernel, n, per_peer, capacity), o...  7.65 us

profile of v5, /device:TPU:1, one launch (start us, length us, event | category | flops | bytes accessed | tf_op | source)
XLA Modules:
  0.0 69.5 jit_solution(2159200214184178919)
XLA Ops:
  0.6 61.3 %exchange.1 = (f32[5248,128]{1,0:T(8,128)S(1)}, s32[128,1,128]{2,1,0:T(1,128)S(1)}, bf16[128,48,128]{2,1,0:T(8,128)(2,1)S(1)}, bf16[128,48,128]{2,1,0:T(8,128)(2,1)S(1)}, f32[128,128]{1,0:T(8,128)S(1)}) custom-call(bf16[128,128]{1,0:T(8,128)(2,1)} %tf_hbm.1, f32[1,2048]{1,0:T(1,128)} %bitcast.12, f32[1,128]{1,0:T(1,128)} %bitcast.15, s32[1,2048]{1,0:T(1,128)} %bitcast.13, ...), custom_call_target="tpu_custom_call" | custom-call | tf_op jit(solution)/shard_map/exchange/pallas_call | solution.py:407
  61.9 7.6 %finish.1 = (f32[5120,128]{1,0:T(8,128)}, f32[128,128]{1,0:T(8,128)}) custom-call(s32[128,1,128]{2,1,0:T(1,128)S(1)} %get-tuple-element.7.slots_hbm, f32[5248,128]{1,0:T(8,128)S(1)} %get-tuple-element.8.fresh_ref, bf16[6144,128]{1,0:T(8,128)(2,1)S(1)} %bitcast.8, bf16[6144,128]{1,0:T(8,128)(2,1)S(1)} %bitcast.9, f32[128,128]{1,0:T(8,128)S(1)} %get-tuple-element.11.counts_ref), custom_call_target="tpu_custom_call" | custom-call | tf_op jit(solution)/shard_map/finish/pallas_call | solution.py:458
